TPU v7x, 32 devices: a whole 2x2x4 slice. The times are simulated.
32 devices in a mesh: section: 2 (over core), dp: 4 (over y, x), tensor: 4 (over z).
Axes of the slice: x: 2, y: 2, z: 4, core: 2. Of those that a mesh axis runs over, the one named last changes fastest.
Arguments:
- tokens_in: bfloat16 [512, 8192], P('dp', ('section', 'tensor')), may hold values from -70 to 70
- gain_attn: bfloat16 [8192], replicated, may hold values from 0.5 to 1.5
- w_query: bfloat16 [8192, 8192], P(None, ('section', 'tensor')), may hold values from -6 to 6
- w_keyval: bfloat16 [8192, 2048], P(None, ('section', 'tensor')), may hold values from -0.0625 to 0.0625
- w_out: bfloat16 [8192, 8192], P(('section', 'tensor')), may hold values from -0.0625 to 0.0625
- gain_mlp: bfloat16 [8192], replicated, may hold values from 0.5 to 1.5
- w_gate: bfloat16 [8192, 16384], P('dp', ('section', 'tensor')), may hold values from -0.0625 to 0.0625
- w_up: bfloat16 [8192, 16384], P('dp', ('section', 'tensor')), may hold values from -0.0625 to 0.0625
- w_down: bfloat16 [16384, 8192], P(('section', 'tensor'), 'dp'), may hold values from -0.046875 to 0.046875
Outputs:
- layer_out: bfloat16 [512, 8192], P(('section', 'tensor'), 'dp')
All inputs are finite; a program needn't handle non-finite values.
Results may differ from a plain program's by a relative error of at most 0.0068.
Values may be sent and summed in bfloat16 or wider, within the bound.
A program may use at most 128 MiB of HBM per device.

v0:
```python
import jax
import jax.numpy as jnp
from jax import lax
from jax.sharding import PartitionSpec as P

H = 64
KVH = 8
HD = 128
EPS = 1e-05
THETA = 10000.0


def rms_scale(row_data, gain_row):
    values = row_data.astype(jnp.float32)
    factor = lax.rsqrt(jnp.mean(values * values, axis=-1, keepdims=True) + EPS)
    return (values * factor * gain_row.astype(jnp.float32)).astype(jnp.bfloat16)


def rotary(values, positions):
    half_dim = values.shape[-1] // 2
    frequency = THETA ** (-jnp.arange(half_dim, dtype=jnp.float32) * 2.0 / values.shape[-1])
    angles = positions.astype(jnp.float32)[:, None] * frequency[None, :]
    cosine = jnp.cos(angles)[:, None, :]
    sine_part = jnp.sin(angles)[:, None, :]
    first_half = values[..., :half_dim]
    second = values[..., half_dim:]
    return jnp.concatenate(
        [first_half * cosine - second * sine_part, second * cosine + first_half * sine_part],
        axis=-1,
    )


def shards(tokens_in, gain_attn, w_query, w_keyval, w_out, gain_mlp, w_gate, w_up, w_down):
    group_count = lax.axis_size(("section", "tensor"))
    group_index = lax.axis_index(("section", "tensor"))
    data_index = lax.axis_index("dp")
    local_rows = tokens_in.shape[0]
    full_rows = lax.all_gather(tokens_in, ("section", "tensor"), axis=1, tiled=True)
    normed_attn = rms_scale(full_rows, gain_attn)
    heads_dev = w_query.shape[1] // HD
    group_size = H // KVH
    kv_dev = max(1, heads_dev // group_size)
    positions_local = data_index * local_rows + jnp.arange(local_rows, dtype=jnp.int32)
    query_proj = jnp.dot(normed_attn, w_query, preferred_element_type=jnp.float32)
    query_rot = rotary(query_proj.reshape(local_rows, heads_dev, HD), positions_local).astype(
        jnp.bfloat16
    )
    keyval_part = jnp.dot(normed_attn, w_keyval, preferred_element_type=jnp.float32).astype(
        jnp.bfloat16
    )
    keyval_rows = lax.all_gather(keyval_part, ("section", "tensor"), axis=1, tiled=True)
    first_kv = group_index * heads_dev // group_size
    key_cols = lax.dynamic_slice_in_dim(keyval_rows, first_kv * HD, kv_dev * HD, 1)
    value_cols = lax.dynamic_slice_in_dim(keyval_rows, KVH * HD + first_kv * HD, kv_dev * HD, 1)
    needed = jnp.concatenate([key_cols, value_cols], axis=1)
    kv_all = lax.all_gather(needed, "dp", axis=0, tiled=True)
    total_rows = kv_all.shape[0]
    key_pos = jnp.arange(total_rows, dtype=jnp.int32)
    key_rot = rotary(
        kv_all[:, : kv_dev * HD].astype(jnp.float32).reshape(total_rows, kv_dev, HD), key_pos
    ).astype(jnp.bfloat16)
    value_all = kv_all[:, kv_dev * HD :].reshape(total_rows, kv_dev, HD)
    query_grp = query_rot.reshape(local_rows, kv_dev, heads_dev // kv_dev, HD)
    scores = jnp.einsum(
        "rkgd,skd->kgrs", query_grp, key_rot, preferred_element_type=jnp.float32
    ) * HD ** (-0.5)
    allowed = key_pos[None, :] <= positions_local[:, None]
    scores = jnp.where(allowed[None, None, :, :], scores, -1e30)
    row_peak = jnp.max(scores, axis=-1, keepdims=True)
    expo_rows = jnp.exp(scores - row_peak)
    prob_rows = (expo_rows / jnp.sum(expo_rows, axis=-1, keepdims=True)).astype(jnp.bfloat16)
    attended = jnp.einsum(
        "kgrs,skd->rkgd", prob_rows, value_all, preferred_element_type=jnp.float32
    )
    attended = attended.astype(jnp.bfloat16).reshape(local_rows, heads_dev * HD)
    head_terms = jnp.dot(attended, w_out, preferred_element_type=jnp.float32)
    summed = lax.psum(head_terms, ("section", "tensor"))
    mid_full = (full_rows.astype(jnp.float32) + summed).astype(jnp.bfloat16)
    normed_mlp = rms_scale(mid_full, gain_mlp)
    mid_cols, norm_cols = (
        lax.all_to_all(mid_full, "dp", split_axis=1, concat_axis=0, tiled=True),
        lax.all_to_all(normed_mlp, "dp", split_axis=1, concat_axis=0, tiled=True),
    )
    hidden_width = w_gate.shape[1]
    row_block = norm_cols
    gate_block = jnp.dot(row_block, w_gate, preferred_element_type=jnp.float32)
    up_block = jnp.dot(row_block, w_up, preferred_element_type=jnp.float32)
    gate_both = lax.psum_scatter(
        jnp.concatenate([gate_block, up_block], axis=1), "dp", scatter_dimension=0, tiled=True
    )
    hidden_part = (jax.nn.silu(gate_both[:, :hidden_width]) * gate_both[:, hidden_width:]).astype(
        jnp.bfloat16
    )
    hidden_all = lax.all_gather(hidden_part, "dp", axis=0, tiled=True)
    out_rows = hidden_all.shape[0] // group_count
    row_block = hidden_all
    down_part = lax.psum_scatter(
        jnp.dot(row_block, w_down, preferred_element_type=jnp.float32),
        ("section", "tensor"),
        scatter_dimension=0,
        tiled=True,
    )
    resid_rows = lax.dynamic_slice_in_dim(mid_cols, group_index * out_rows, out_rows, 0)
    return (resid_rows.astype(jnp.float32) + down_part).astype(jnp.bfloat16)


def solution(mesh):
    placed = (
        P("dp", ("section", "tensor")),
        P(),
        P(None, ("section", "tensor")),
        P(None, ("section", "tensor")),
        P(("section", "tensor"), None),
        P(),
        P("dp", ("section", "tensor")),
        P("dp", ("section", "tensor")),
        P(("section", "tensor"), "dp"),
    )
    return jax.shard_map(
        shards,
        mesh=mesh,
        in_specs=placed,
        out_specs=P(("section", "tensor"), "dp"),
        check_vma=False,
    )
```

profile of v0, /device:TPU:0, one launch (start us, length us, event | category | flops | bytes accessed | tf_op | source)
XLA Modules:
  0.0 471.4 jit_solution(17559355887173237044)
XLA Ops:
  6.5 0.0 all-gather.3.cloned.1.call-start
  6.5 0.7 all-gather.3.cloned.1.call-update
  7.3 0.0 all-reduce.2.cloned.1.call-start
  7.3 0.7 convert_element_type.75
  8.1 0.3 multiply_cosine_fusion.1
  8.5 32.4 %all-gather.3.cloned.1.call-done = bf16[128,8192]{1,0:T(8,128)(2,1)} async-done(((bf16[128,1024]{1,0:T(8,128)(2,1)}), bf16[128,8192]{1,0:T(8,128)(2,1)}) %all-gather.3.cloned.1.call-update) | async-done | bytes 2097168 | tf_op jit(solution)/shard_map/all_gather | solution.py:38
  40.8 2.1 fusion.3
  42.9 0.0 copy-start
  42.9 3.7 convolution_convert_fusion.1
  46.7 26.2 %all_gather.13 = bf16[128,2048]{1,0:T(8,128)(2,1)S(1)} all-gather(bf16[128,256]{1,0:T(8,128)(2,1)S(1)} %convolution_convert_fusion.1), channel_id=1, replica_groups=mesh['section'=2,'dp'=4,'tensor'=4] {'section','tensor'}, dimensions={1}, use_global_device_ids=true | all-gather | bytes 589824 | tf_op jit(solution)/shard_map/all_gather | solution.py:51
  72.9 9.0 %all_gather.14 = bf16[512,256]{1,0:T(8,128)(2,1)S(1)} all-gather(bf16[128,256]{1,0:T(8,128)(2,1)S(1)} %pad_maximum_fusion.1), channel_id=1, replica_groups=mesh['section'=2,'dp'=4,'tensor'=4] {'dp'}, dimensions={0}, use_global_device_ids=true | all-gather | bytes 327680 | tf_op jit(solution)/shard_map/all_gather | solution.py:56
  81.9 0.0 copy-done
  81.9 0.0 slice-start
  81.9 0.0 slice-start.1
  81.9 0.0 slice-start.2
  81.9 8.4 %convolution_bitcast_fusion = f32[16,8,8,128]{3,1,2,0:T(8,128)S(1)} fusion(bf16[8192,1024]{1,0:T(8,128)(2,1)} %param.11, bf16[128,8192]{1,0:T(8,128)(2,1)S(1)} %copy-done, f32[8192]{0:T(1024)S(1)} %convert_element_type.75, f32[128]{0:T(128)S(1)} %add_rsqrt_fusion.1), kind=kOutput, calls=%fused_computation.19 | convolution fusion | flops 2151677952 | bytes 19431936 | tf_op jit(solution)/shard_map/dot_general | solution.py:44
  90.4 0.1 copy.34
  90.5 0.2 fusion.31
  90.7 1.2 fusion.27
  91.9 0.2 subtract_convert_fusion
  92.1 0.0 slice-start.3
  92.1 0.6 fusion.32
  92.7 0.3 fusion.7
  93.0 0.5 convolution_convert_fusion
  93.5 0.0 slice-done
  93.5 0.0 slice-done.1
  93.5 0.0 slice-done.2
  93.6 0.7 slice-done.3
  94.3 4.8 %fusion.33 = f32[128,8192]{1,0:T(8,128)} fusion(bf16[128,1024]{0,1:T(8,128)(2,1)S(1)} %bitcast.66, bf16[1024,8192]{1,0:T(8,128)(2,1)S(1)} %bitcast.58), kind=kOutput, calls=%fused_computation.64 | convolution fusion | flops 2147483648 | bytes 21233664 | tf_op jit(solution)/shard_map/dot_general | solution.py:76
  99.1 0.0 copy-start.1
  99.1 0.0 all-reduce.2.cloned.1.call-update
  99.2 0.0 reduce-scatter.3.cloned.1.call-start
  99.2 0.6 copy-done.1
  99.9 94.9 %all-reduce.2.cloned.1.call-done = f32[128,8192]{1,0:T(8,128)} async-done(((f32[128,8192]{1,0:T(8,128)}), f32[128,8192]{1,0:T(8,128)}) %all-reduce.2.cloned.1.call-update) | async-done | bytes 4194320 | tf_op jit(solution)/shard_map/psum | solution.py:77
  194.8 0.0 slice-start.4
  194.8 3.7 fusion
  198.5 0.0 slice-start.5
  198.5 0.6 fusion.2
  199.2 0.2 copy.41
  199.4 0.0 slice-start.6
  199.4 28.8 %all_to_all.38 = bf16[128,4,2048]{2,0,1:T(8,128)(2,1)S(1)} all-to-all(bf16[128,4,2048]{2,0,1:T(8,128)(2,1)S(1)} %bitcast.61), channel_id=1, replica_groups=mesh['section'=2,'dp'=4,'tensor'=4] {'dp'}, dimensions={1} | all-to-all | bytes 4194304 | tf_op jit(solution)/shard_map/all_to_all | solution.py:82
  228.3 0.0 slice-done.4
  228.3 0.0 slice-done.5
  228.3 0.0 slice-start.7
  228.3 4.6 fusion.35
  232.9 0.0 slice-done.6
  232.9 0.0 slice-done.7
  232.9 4.6 fusion.34
  237.5 3.8 pad_maximum_fusion
  241.3 0.0 reduce-scatter.3.cloned.1.call-update
  241.3 0.0 all-gather.5.cloned.1.call-start
  241.4 85.1 %reduce-scatter.3.cloned.1.call-done = f32[128,4096]{1,0:T(8,128)} async-done(((f32[512,4096]{1,0:T(8,128)}), f32[128,4096]{1,0:T(8,128)}) %reduce-scatter.3.cloned.1.call-update) | async-done | bytes 2097168 | tf_op jit(solution)/shard_map/reduce_scatter | solution.py:88
  326.5 2.6 fusion.8
  329.1 0.0 all-gather.5.cloned.1.call-update
  329.1 0.0 reduce-scatter.5.cloned.1.call-start
  329.2 35.3 %all-gather.5.cloned.1.call-done = bf16[512,2048]{1,0:T(8,128)(2,1)} async-done(((bf16[128,2048]{1,0:T(8,128)(2,1)}), bf16[512,2048]{1,0:T(8,128)(2,1)}) %all-gather.5.cloned.1.call-update) | async-done | bytes 2097168 | tf_op jit(solution)/shard_map/all_gather | solution.py:94
  364.5 10.5 %fusion.36 = f32[512,2048]{1,0:T(8,128)} fusion(bf16[512,2048]{1,0:T(8,128)(2,1)} %all-gather.5.cloned.1.call-done, bf16[2048,2048]{1,0:T(8,128)(2,1)} %param.17), kind=kOutput, calls=%fused_computation.67 | convolution fusion | flops 4294967296 | bytes 14680064 | tf_op jit(solution)/shard_map/dot_general | solution.py:98
  374.9 0.0 reduce-scatter.5.cloned.1.call-update
  374.9 1.5 copy.42
  376.4 3.6 all-to-all-start
  380.0 24.9 %all-to-all-done = bf16[128,4,2048]{2,0,1:T(8,128)(2,1)S(1)} async-done(((bf16[128,4,2048]{2,0,1:T(8,128)(2,1)}), bf16[128,4,2048]{2,0,1:T(8,128)(2,1)S(1)}, u32[]{:S(2)}, u32[]{:S(2)}) %all-to-all-start) | async-done | bytes 2097184 | tf_op jit(solution)/shard_map/all_to_all | solution.py:81
  405.0 58.1 %reduce-scatter.5.cloned.1.call-done = f32[64,2048]{1,0:T(8,128)} async-done(((f32[512,2048]{1,0:T(8,128)}), f32[64,2048]{1,0:T(8,128)}) %reduce-scatter.5.cloned.1.call-update) | async-done | bytes 524304 | tf_op jit(solution)/shard_map/reduce_scatter | solution.py:97
  463.1 1.8 add_convert_fusion
  (14 shorter events, 0.1 us)
Async XLA Ops:
  6.5 34.3 %all-gather.3.cloned.1.call-start = ((), (), s32[]{:S(2)}) async-start(), calls=%async_computation.4 | async-start | bytes 2359296 | tf_op jit(solution)/shard_map/all_gather | solution.py:38
  7.3 187.5 %all-reduce.2.cloned.1.call-start = ((), (), s32[]{:S(2)}) async-start(), calls=%async_computation.5 | async-start | bytes 8388608 | tf_op jit(solution)/shard_map/psum | solution.py:77
  42.9 39.0 %copy-start = (bf16[128,8192]{1,0:T(8,128)(2,1)S(1)}, bf16[128,8192]{1,0:T(8,128)(2,1)}, u32[]{:S(2)}) copy-start(bf16[128,8192]{1,0:T(8,128)(2,1)} %all-gather.3.cloned.1.call-done) | copy-start | bytes 6291460
  81.9 11.6 %slice-start = ((s8[16777216]{0:T(1024)(128)(4,1)}), s8[4194304]{0:T(1024)(128)(4,1)S(1)}, s32[]{:S(2)}) async-start(s8[16777216]{0:T(1024)(128)(4,1)} %bitcast.57), calls=%async_computation.9 | async-start | bytes 8388608
  81.9 11.6 %slice-start.1 = ((s8[16777216]{0:T(1024)(128)(4,1)}), s8[4194304]{0:T(1024)(128)(4,1)S(1)}, s32[]{:S(2)}) async-start(s8[16777216]{0:T(1024)(128)(4,1)} %bitcast.57), calls=%async_computation.10 | async-start | bytes 8388608
  81.9 11.6 %slice-start.2 = ((s8[16777216]{0:T(1024)(128)(4,1)}), s8[4194304]{0:T(1024)(128)(4,1)S(1)}, s32[]{:S(2)}) async-start(s8[16777216]{0:T(1024)(128)(4,1)} %bitcast.57), calls=%async_computation.11 | async-start | bytes 8388608
  92.1 2.2 slice-start.3
  99.1 0.7 copy-start.1
  99.2 227.3 %reduce-scatter.3.cloned.1.call-start = ((), (), s32[]{:S(2)}) async-start(), calls=%async_computation.6 | async-start | bytes 10485760 | tf_op jit(solution)/shard_map/reduce_scatter | solution.py:88
  194.8 33.5 %slice-start.4 = ((s8[8388608]{0:T(1024)(128)(4,1)}), s8[4194304]{0:T(1024)(128)(4,1)S(1)}, s32[]{:S(2)}) async-start(s8[8388608]{0:T(1024)(128)(4,1)} %bitcast.67), calls=%async_computation.13 | async-start | bytes 8388608
  198.5 29.8 %slice-start.5 = ((s8[8388608]{0:T(1024)(128)(4,1)}), s8[4194304]{0:T(1024)(128)(4,1)S(1)}, s32[]{:S(2)}) async-start(s8[8388608]{0:T(1024)(128)(4,1)} %bitcast.67), calls=%async_computation.14 | async-start | bytes 8388608
  199.4 33.5 %slice-start.6 = ((s8[8388608]{0:T(1024)(128)(4,1)}), s8[4194304]{0:T(1024)(128)(4,1)S(1)}, s32[]{:S(2)}) async-start(s8[8388608]{0:T(1024)(128)(4,1)} %bitcast.69), calls=%async_computation.15 | async-start | bytes 8388608
  228.3 4.6 slice-start.7
  241.3 123.2 %all-gather.5.cloned.1.call-start = ((), (), s32[]{:S(2)}) async-start(), calls=%async_computation.7 | async-start | bytes 2621440 | tf_op jit(solution)/shard_map/all_gather | solution.py:94
  329.1 133.9 %reduce-scatter.5.cloned.1.call-start = ((), (), s32[]{:S(2)}) async-start(), calls=%async_computation.8 | async-start | bytes 4718592 | tf_op jit(solution)/shard_map/reduce_scatter | solution.py:97
  376.4 28.6 %all-to-all-start = ((bf16[128,4,2048]{2,0,1:T(8,128)(2,1)}), bf16[128,4,2048]{2,0,1:T(8,128)(2,1)S(1)}, u32[]{:S(2)}, u32[]{:S(2)}) async-start(bf16[128,4,2048]{2,0,1:T(8,128)(2,1)} %bitcast.59), calls=%async_computation | async-start | bytes 4194304 | tf_op jit(solution)/shard_map/all_to_all | solution.py:81
Sparse Core Ops, SparseCore 0:
  8.9 31.8 all-gather.2
  99.3 95.4 all-reduce.1
  241.4 85.0 reduce-scatter.2
  329.3 35.1 all-gather.4
  375.1 87.9 reduce-scatter.4
where the time goes:
time: 472 us; the launch traced here: 471 us
  waiting for transfers between devices  332 us (70%)
  blocking collectives  64 us (14%)
  matrix products  37.7 us (8%)
  other arithmetic  17.5 us (4%)
  between operations  13.5 us (3%)
    psum x1, waiting for transfers between devices, shards(): summed = lax.psum(head_terms, ('section', 'tensor'))  94.9 us
    reduce_scatter x1, waiting for transfers between devices, shards(): lax.psum_scatter(jnp.concatenate([gate_block, up_block], axis=1), 'dp', s...  85.1 us
    reduce_scatter x1, waiting for transfers between devices, shards(): lax.psum_scatter(jnp.dot(row_block, w_down, preferred_element_type=jnp.fl...  58.1 us
    all_gather x1, waiting for transfers between devices, shards(): hidden_all = lax.all_gather(hidden_part, 'dp', axis=0, tiled=True)  35.3 us
    all_gather x1, waiting for transfers between devices, shards(): lax.all_gather(tokens_in, ('section', 'tensor'), axis=1, tiled=True)  32.4 us
    all_to_all x1, blocking collectives, shards(): lax.all_to_all(normed_mlp, 'dp', split_axis=1, concat_axis=0, tiled=True)  28.8 us
    all_gather x1, blocking collectives, shards(): lax.all_gather(keyval_part, ('section', 'tensor'), axis=1, tiled=True)  26.2 us
    all_to_all x1, waiting for transfers between devices, shards(): lax.all_to_all(mid_full, 'dp', split_axis=1, concat_axis=0, tiled=True)  24.9 us
  transfers between devices with their start and end apart: 6, of which 6 were waited for; matrix products, arithmetic and copies ran while one was open for 1% of the time, Pallas kernels for 0%

commit v1 on v0

--- a/solution.py
+++ b/solution.py
@@ -74,7 +74,7 @@
     )
     attended = attended.astype(jnp.bfloat16).reshape(local_rows, heads_dev * HD)
     head_terms = jnp.dot(attended, w_out, preferred_element_type=jnp.float32)
-    summed = lax.psum(head_terms, ("section", "tensor"))
+    summed = lax.psum(lax.psum(head_terms, "tensor"), "section")
     mid_full = (full_rows.astype(jnp.float32) + summed).astype(jnp.bfloat16)
     normed_mlp = rms_scale(mid_full, gain_mlp)
     mid_cols, norm_cols = (

time: 472 us -> 562 us (1.19)
  waiting for transfers between devices: 332 us -> 421 us
    psum x1 -> x2, waiting for transfers between devices: 94.9 us -> 184 us  [shards(): summed = lax.psum(lax.psum(head_terms, 'tensor'), 'section')]
  transfers between devices with their start and end apart: 6 -> 7, of which waited for: 6 -> 7; matrix products, arithmetic and copies ran while one was open for 1% -> 0% of each run, Pallas kernels for 0% -> 0%
where the time goes in v1:
time: 562 us
  waiting for transfers between devices  421 us (75%)
  blocking collectives  65 us (12%)
  matrix products  37.7 us (7%)
  other arithmetic  17.5 us (3%)
  between operations  13.8 us (2%)
    psum x2, waiting for transfers between devices, shards(): summed = lax.psum(lax.psum(head_terms, 'tensor'), 'section')  184 us
    reduce_scatter x1, waiting for transfers between devices, shards(): lax.psum_scatter(jnp.concatenate([gate_block, up_block], axis=1), 'dp', s...  85.8 us
    reduce_scatter x1, waiting for transfers between devices, shards(): lax.psum_scatter(jnp.dot(row_block, w_down, preferred_element_type=jnp.fl...  58.1 us
    all_gather x1, waiting for transfers between devices, shards(): hidden_all = lax.all_gather(hidden_part, 'dp', axis=0, tiled=True)  35.3 us
    all_gather x1, waiting for transfers between devices, shards(): lax.all_gather(tokens_in, ('section', 'tensor'), axis=1, tiled=True)  32.4 us
    all_to_all x1, blocking collectives, shards(): lax.all_to_all(normed_mlp, 'dp', split_axis=1, concat_axis=0, tiled=True)  29.8 us
    all_gather x1, blocking collectives, shards(): lax.all_gather(keyval_part, ('section', 'tensor'), axis=1, tiled=True)  26.2 us
    all_to_all x1, waiting for transfers between devices, shards(): lax.all_to_all(mid_full, 'dp', split_axis=1, concat_axis=0, tiled=True)  24.9 us
  transfers between devices with their start and end apart: 7, of which 7 were waited for; matrix products, arithmetic and copies ran while one was open for 0% of the time, Pallas kernels for 0%

profile of v1, /device:TPU:0, one launch (start us, length us, event | category | flops | bytes accessed | tf_op | source)
XLA Modules:
  0.0 561.7 jit_solution(19320388560933179)
XLA Ops:
  6.5 0.0 all-gather.3.cloned.1.call-start
  6.5 0.7 all-gather.3.cloned.1.call-update
  7.3 0.0 all-reduce.3.cloned.1.call-start
  7.3 0.7 convert_element_type.75
  8.1 0.3 multiply_cosine_fusion.1
  8.5 32.4 %all-gather.3.cloned.1.call-done = bf16[128,8192]{1,0:T(8,128)(2,1)} async-done(((bf16[128,1024]{1,0:T(8,128)(2,1)}), bf16[128,8192]{1,0:T(8,128)(2,1)}) %all-gather.3.cloned.1.call-update) | async-done | bytes 2097168 | tf_op jit(solution)/shard_map/all_gather | solution.py:38
  40.8 2.1 fusion.3
  42.9 0.0 copy-start
  42.9 3.7 convolution_convert_fusion.1
  46.7 26.2 %all_gather.13 = bf16[128,2048]{1,0:T(8,128)(2,1)S(1)} all-gather(bf16[128,256]{1,0:T(8,128)(2,1)S(1)} %convolution_convert_fusion.1), channel_id=1, replica_groups=mesh['section'=2,'dp'=4,'tensor'=4] {'section','tensor'}, dimensions={1}, use_global_device_ids=true | all-gather | bytes 589824 | tf_op jit(solution)/shard_map/all_gather | solution.py:51
  72.9 9.0 %all_gather.14 = bf16[512,256]{1,0:T(8,128)(2,1)S(1)} all-gather(bf16[128,256]{1,0:T(8,128)(2,1)S(1)} %pad_maximum_fusion.1), channel_id=1, replica_groups=mesh['section'=2,'dp'=4,'tensor'=4] {'dp'}, dimensions={0}, use_global_device_ids=true | all-gather | bytes 327680 | tf_op jit(solution)/shard_map/all_gather | solution.py:56
  81.9 0.0 copy-done
  81.9 0.0 slice-start
  81.9 0.0 slice-start.1
  81.9 0.0 slice-start.2
  81.9 8.4 %convolution_bitcast_fusion = f32[16,8,8,128]{3,1,2,0:T(8,128)S(1)} fusion(bf16[8192,1024]{1,0:T(8,128)(2,1)} %param.11, bf16[128,8192]{1,0:T(8,128)(2,1)S(1)} %copy-done, f32[8192]{0:T(1024)S(1)} %convert_element_type.75, f32[128]{0:T(128)S(1)} %add_rsqrt_fusion.1), kind=kOutput, calls=%fused_computation.19 | convolution fusion | flops 2151677952 | bytes 19431936 | tf_op jit(solution)/shard_map/dot_general | solution.py:44
  90.4 0.1 copy.34
  90.5 0.2 fusion.31
  90.7 1.2 fusion.27
  91.9 0.2 subtract_convert_fusion
  92.1 0.0 slice-start.3
  92.1 0.6 fusion.32
  92.7 0.3 fusion.7
  93.0 0.5 convolution_convert_fusion
  93.5 0.0 slice-done
  93.5 0.0 slice-done.1
  93.5 0.0 slice-done.2
  93.6 0.7 slice-done.3
  94.3 4.8 fusion.33
  99.1 0.0 copy-start.1
  99.1 0.0 all-reduce.3.cloned.1.call-update
  99.2 0.0 all-reduce.5.cloned.1.call-start
  99.2 154.1 %all-reduce.3.cloned.1.call-done = f32[128,8192]{1,0:T(8,128)} async-done(((f32[128,8192]{1,0:T(8,128)}), f32[128,8192]{1,0:T(8,128)}) %all-reduce.3.cloned.1.call-update) | async-done | bytes 4194320 | tf_op jit(solution)/shard_map/psum | solution.py:77
  253.3 0.0 all-reduce.5.cloned.1.call-update
  253.3 0.0 reduce-scatter.3.cloned.1.call-start
  253.4 0.0 copy-done.1
  253.4 29.6 %all-reduce.5.cloned.1.call-done = f32[128,8192]{1,0:T(8,128)} async-done(((f32[128,8192]{1,0:T(8,128)}), f32[128,8192]{1,0:T(8,128)}) %all-reduce.5.cloned.1.call-update) | async-done | bytes 4194320 | tf_op jit(solution)/shard_map/psum | solution.py:77
  283.0 3.7 fusion
  286.8 0.0 slice-start.5
  286.8 0.6 fusion.2
  287.4 0.2 copy.41
  287.7 0.0 slice-start.6
  287.7 29.8 %all_to_all.38 = bf16[128,4,2048]{2,0,1:T(8,128)(2,1)S(1)} all-to-all(bf16[128,4,2048]{2,0,1:T(8,128)(2,1)S(1)} %bitcast.61), channel_id=1, replica_groups=mesh['section'=2,'dp'=4,'tensor'=4] {'dp'}, dimensions={1} | all-to-all | bytes 4194304 | tf_op jit(solution)/shard_map/all_to_all | solution.py:82
  317.5 0.0 slice-done.4
  317.5 0.0 slice-done.5
  317.5 4.6 fusion.35
  322.1 0.0 slice-done.6
  322.1 0.0 slice-done.7
  322.1 4.6 fusion.34
  326.7 3.8 pad_maximum_fusion
  330.5 0.0 reduce-scatter.3.cloned.1.call-update
  330.5 0.0 all-gather.5.cloned.1.call-start
  330.6 85.8 %reduce-scatter.3.cloned.1.call-done = f32[128,4096]{1,0:T(8,128)} async-done(((f32[512,4096]{1,0:T(8,128)}), f32[128,4096]{1,0:T(8,128)}) %reduce-scatter.3.cloned.1.call-update) | async-done | bytes 2097168 | tf_op jit(solution)/shard_map/reduce_scatter | solution.py:88
  416.4 2.6 fusion.8
  419.0 0.0 all-gather.5.cloned.1.call-update
  419.1 0.0 reduce-scatter.5.cloned.1.call-start
  419.1 35.3 %all-gather.5.cloned.1.call-done = bf16[512,2048]{1,0:T(8,128)(2,1)} async-done(((bf16[128,2048]{1,0:T(8,128)(2,1)}), bf16[512,2048]{1,0:T(8,128)(2,1)}) %all-gather.5.cloned.1.call-update) | async-done | bytes 2097168 | tf_op jit(solution)/shard_map/all_gather | solution.py:94
  454.4 10.5 %fusion.36 = f32[512,2048]{1,0:T(8,128)} fusion(bf16[512,2048]{1,0:T(8,128)(2,1)} %all-gather.5.cloned.1.call-done, bf16[2048,2048]{1,0:T(8,128)(2,1)} %param.17), kind=kOutput, calls=%fused_computation.67 | convolution fusion | flops 4294967296 | bytes 14680064 | tf_op jit(solution)/shard_map/dot_general | solution.py:98
  464.9 0.0 reduce-scatter.5.cloned.1.call-update
  464.9 1.5 copy.42
  466.4 3.6 all-to-all-start
  470.0 24.9 %all-to-all-done = bf16[128,4,2048]{2,0,1:T(8,128)(2,1)S(1)} async-done(((bf16[128,4,2048]{2,0,1:T(8,128)(2,1)}), bf16[128,4,2048]{2,0,1:T(8,128)(2,1)S(1)}, u32[]{:S(2)}, u32[]{:S(2)}) %all-to-all-start) | async-done | bytes 2097184 | tf_op jit(solution)/shard_map/all_to_all | solution.py:81
  494.9 58.1 %reduce-scatter.5.cloned.1.call-done = f32[64,2048]{1,0:T(8,128)} async-done(((f32[512,2048]{1,0:T(8,128)}), f32[64,2048]{1,0:T(8,128)}) %reduce-scatter.5.cloned.1.call-update) | async-done | bytes 524304 | tf_op jit(solution)/shard_map/reduce_scatter | solution.py:97
  553.0 1.8 add_convert_fusion
  (16 shorter events, 0.1 us)
Async XLA Ops:
  6.5 34.3 %all-gather.3.cloned.1.call-start = ((), (), s32[]{:S(2)}) async-start(), calls=%async_computation.4 | async-start | bytes 2359296 | tf_op jit(solution)/shard_map/all_gather | solution.py:38
  7.3 246.0 %all-reduce.3.cloned.1.call-start = ((), (), s32[]{:S(2)}) async-start(), calls=%async_computation.5 | async-start | bytes 8388608 | tf_op jit(solution)/shard_map/psum | solution.py:77
  42.9 39.0 %copy-start = (bf16[128,8192]{1,0:T(8,128)(2,1)S(1)}, bf16[128,8192]{1,0:T(8,128)(2,1)}, u32[]{:S(2)}) copy-start(bf16[128,8192]{1,0:T(8,128)(2,1)} %all-gather.3.cloned.1.call-done) | copy-start | bytes 6291460
  81.9 11.6 %slice-start = ((s8[16777216]{0:T(1024)(128)(4,1)}), s8[4194304]{0:T(1024)(128)(4,1)S(1)}, s32[]{:S(2)}) async-start(s8[16777216]{0:T(1024)(128)(4,1)} %bitcast.57), calls=%async_computation.10 | async-start | bytes 8388608
  81.9 11.6 %slice-start.1 = ((s8[16777216]{0:T(1024)(128)(4,1)}), s8[4194304]{0:T(1024)(128)(4,1)S(1)}, s32[]{:S(2)}) async-start(s8[16777216]{0:T(1024)(128)(4,1)} %bitcast.57), calls=%async_computation.11 | async-start | bytes 8388608
  81.9 11.6 %slice-start.2 = ((s8[16777216]{0:T(1024)(128)(4,1)}), s8[4194304]{0:T(1024)(128)(4,1)S(1)}, s32[]{:S(2)}) async-start(s8[16777216]{0:T(1024)(128)(4,1)} %bitcast.57), calls=%async_computation.12 | async-start | bytes 8388608
  92.1 2.2 slice-start.3
  99.1 154.2 %copy-start.1 = (bf16[8192]{0:T(1024)(128)(2,1)S(1)}, bf16[8192]{0:T(1024)(128)(2,1)}, u32[]{:S(2)}) copy-start(bf16[8192]{0:T(1024)(128)(2,1)} %param.14) | copy-start | bytes 49156
  99.2 183.9 %all-reduce.5.cloned.1.call-start = ((), (), s32[]{:S(2)}) async-start(), calls=%async_computation.6 | async-start | bytes 8388608 | tf_op jit(solution)/shard_map/psum | solution.py:77
  253.3 163.1 %reduce-scatter.3.cloned.1.call-start = ((), (), s32[]{:S(2)}) async-start(), calls=%async_computation.7 | async-start | bytes 10485760 | tf_op jit(solution)/shard_map/reduce_scatter | solution.py:88
  283.0 34.5 %slice-start.4 = ((s8[8388608]{0:T(1024)(128)(4,1)}), s8[4194304]{0:T(1024)(128)(4,1)S(1)}, s32[]{:S(2)}) async-start(s8[8388608]{0:T(1024)(128)(4,1)} %bitcast.67), calls=%async_computation.14 | async-start | bytes 8388608
  286.8 30.7 %slice-start.5 = ((s8[8388608]{0:T(1024)(128)(4,1)}), s8[4194304]{0:T(1024)(128)(4,1)S(1)}, s32[]{:S(2)}) async-start(s8[8388608]{0:T(1024)(128)(4,1)} %bitcast.67), calls=%async_computation.15 | async-start | bytes 8388608
  287.7 34.4 %slice-start.6 = ((s8[8388608]{0:T(1024)(128)(4,1)}), s8[4194304]{0:T(1024)(128)(4,1)S(1)}, s32[]{:S(2)}) async-start(s8[8388608]{0:T(1024)(128)(4,1)} %bitcast.69), calls=%async_computation.16 | async-start | bytes 8388608
  317.5 4.6 slice-start.7
  330.5 123.9 %all-gather.5.cloned.1.call-start = ((), (), s32[]{:S(2)}) async-start(), calls=%async_computation.8 | async-start | bytes 2621440 | tf_op jit(solution)/shard_map/all_gather | solution.py:94
  419.1 134.0 %reduce-scatter.5.cloned.1.call-start = ((), (), s32[]{:S(2)}) async-start(), calls=%async_computation.9 | async-start | bytes 4718592 | tf_op jit(solution)/shard_map/reduce_scatter | solution.py:97
  466.4 28.6 %all-to-all-start = ((bf16[128,4,2048]{2,0,1:T(8,128)(2,1)}), bf16[128,4,2048]{2,0,1:T(8,128)(2,1)S(1)}, u32[]{:S(2)}, u32[]{:S(2)}) async-start(bf16[128,4,2048]{2,0,1:T(8,128)(2,1)} %bitcast.59), calls=%async_computation | async-start | bytes 4194304 | tf_op jit(solution)/shard_map/all_to_all | solution.py:81
Sparse Core Ops, SparseCore 0:
  8.9 31.8 all-gather.2
  99.3 153.9 all-reduce.2
  255.8 27.1 all-reduce.4
  330.6 85.7 reduce-scatter.2
  419.2 35.1 all-gather.4
  465.0 87.9 reduce-scatter.4
